TPU v7x, 32 devices: a whole 2x2x4 slice. The times are simulated.
32 devices in a mesh: seq: 8 (over z, y), chan: 4 (over x, core).
Axes of the slice: x: 2, y: 2, z: 4, core: 2. Of those that a mesh axis runs over, the one named last changes fastest.
Arguments:
- inputs: float32 [1024, 8192], P('seq', 'chan'), may hold values from -6 to 6
- conv_weight: float32 [3, 4, 8192], P(None, None, 'chan'), may hold values from -3 to 3
- conv_bias: float32 [3, 8192], P(None, 'chan'), may hold values from -1 to 1
- cotangent: float32 [1024, 8192], P('seq', 'chan'), may hold values from -6 to 6
Outputs:
- output: float32 [1024, 8192], P('seq', 'chan')
- input_grad: float32 [1024, 8192], P('seq', 'chan')
- weight_grad: float32 [3, 4, 8192], P(None, None, 'chan')
- bias_grad: float32 [3, 8192], P(None, 'chan')
All inputs are finite; a program needn't handle non-finite values.
Results may differ from a plain program's by a relative error of at most 0.0001.
Values sent between devices are 32-bit elements; how exact they have to be, the bound alone decides.
No kernel may reach another device: no remote copies, remote signals or barrier semaphores. Data moves between devices by JAX's collectives and lax.ppermute only.
A program may use at most 64 MiB of HBM per device.

v0:
```python
import functools

import jax
import jax.numpy as jnp
from jax import lax
from jax.experimental import pallas as pl
from jax.experimental.pallas import tpu as pltpu
from jax.sharding import PartitionSpec as P


LANES = 128
SUB = 8
BLOCK = 16


class Plan:
    def __init__(self, n, width, layers, taps):
        self.n, self.width, self.layers, self.taps = n, width, layers, taps
        self.reach = taps - 1
        self.halo = layers * self.reach
        self.late = self.halo - self.reach
        self.cols = width // LANES
        self.groups = self.cols // SUB
        self.top = top = -(-self.halo // SUB) * SUB
        rows = []
        L, R, H = layers, self.reach, self.halo
        rows += [(kind, 0, t) for kind in ("x", "ct") for t in range(H)]
        for l in range(1, L):
            rows += [("a", l, t) for t in range(l * R, H)]
        for l in range(L - 1):
            rows += [("d", l, t) for t in range((l + 1) * R, H)]
            rows += [("d", l, t) for t in range(n - (L - 1 - l) * R, n)]
        for l in range(L):
            low = n - (L - 1 - l) * R
            rows += [("g", l, t) for t in range(H, H + R)]
            rows += [("g", l, t) for t in range(low - R, low)]
        rows += [("out", 0, t) for t in range(H, top)]
        rows += [("grad", 0, t) for t in range(H, top)]
        rows += [("grad", 0, t) for t in range(n - top, n - H)]
        self.state = {key: i for i, key in enumerate(rows)}
        self.acc = len(rows)
        self.state_rows = len(rows) + layers * (taps + 1)


def conv(weights, window):
    total = weights[0] * window[0]
    for k in range(1, len(window)):
        total = total + weights[k] * window[k]
    return total + weights[len(window)] if len(weights) > len(window) else total


def gate(h):
    u = jnp.tanh(h)
    v = 1.0 + u
    act = h * v
    return act, v + act * (1.0 - u)


def interior(p, x_ref, ct_ref, w_ref, b_ref, out_hbm, grad_hbm, st_ref, wb_ref, *scratch):
    L, R, H, K, n = p.layers, p.reach, p.halo, p.taps, p.n
    a_s, d_s = scratch[: L - 1], scratch[L - 1 : 2 * L - 1]
    out_s, grad_s, sem = scratch[2 * L - 1 :]
    blocks = n // BLOCK
    copies = []

    def send(src, dst, first, last, g, i):
        where = (pl.ds(first, last - first), pl.ds(g * SUB * SUB, SUB * SUB), slice(None))
        copies.append(pltpu.make_async_copy(src.at[where], dst.at[where], sem.at[i]))
        copies[-1].start()

    for l in range(L):
        for g in range(p.groups):
            for k in range(K):
                wb_ref[l * (K + 1) + k, g * SUB : (g + 1) * SUB, :] = 0.5 * w_ref[
                    pl.ds((l * p.cols + g * SUB) * K + k, SUB, stride=K), :
                ]
            wb_ref[l * (K + 1) + K, g * SUB : (g + 1) * SUB, :] = 0.5 * b_ref[l, g * SUB : (g + 1) * SUB, :]

    for g in range(p.groups):
        lanes = pl.ds(g * SUB, SUB)

        def tile(base, off):
            return (base // SUB + off // SUB, pl.ds(g * SUB * SUB + off % SUB, SUB, stride=SUB), slice(None))

        wb = [[wb_ref[l * (K + 1) + k, lanes, :] for k in range(K + 1)] for l in range(L)]

        def forward(base, windows, first):
            windows = [list(w) for w in windows]
            for off in range(BLOCK):
                act = x_ref[tile(base, off)]
                for l in range(L):
                    windows[l] = windows[l] + [act]
                    if first and off < (l + 1) * R:
                        break
                    act, d = gate(conv(wb[l], windows[l][-K:]))
                    d_s[l][base + off, lanes, :] = d
                    if l < L - 1:
                        a_s[l][base + off, lanes, :] = act
                    else:
                        out_s[tile(base, off)] = act
            return [w[-R:] for w in windows]

        windows = forward(0, [[]] * L, True)
        lax.fori_loop(
            1, blocks, lambda i, w: forward(pl.multiple_of(i * BLOCK, BLOCK), w, False), windows
        )
        send(out_s, out_hbm, p.top // SUB, n // SUB, g, 3 * g)

        wt = [[wb_ref[l * (K + 1) + k, lanes, :] for k in range(K)] for l in range(L)]

        def backward(base, gs, acc, stop, last):
            gs, acc = [list(v) for v in gs], [list(v) for v in acc]
            acts = {}

            def act_at(l, off):
                if (l, off) not in acts:
                    if l == 0:
                        if off >= 0:
                            acts[l, off] = x_ref[tile(base, off)]
                        else:
                            acts[l, off] = x_ref[tile(base - BLOCK, off + BLOCK)]
                    else:
                        acts[l, off] = a_s[l - 1][base + off, lanes, :]
                return acts[l, off]

            for off in reversed(range(stop, BLOCK)):
                grad = ct_ref[tile(base, off)]
                for l in reversed(range(L)):
                    pre = grad * d_s[l][base + off, lanes, :]
                    gs[l] = ([pre] + gs[l])[:K]
                    for k in range(K):
                        acc[l][k] = acc[l][k] + pre * act_at(l, off - R + k)
                    acc[l][K] = acc[l][K] + pre
                    key = ("g", l, base + off if last or stop else None)
                    if key in p.state:
                        st_ref[p.state[key], lanes, :] = pre
                    if last and base + off >= n - (L - l) * R:
                        break
                    grad = conv(wt[l][::-1], gs[l])
                else:
                    grad_s[tile(base, off)] = grad
            return [v[:R] for v in gs], acc

        zero = jnp.zeros((SUB, LANES), jnp.float32)
        gs, acc = [[]] * L, [[zero] * (K + 1)] * L
        gs, acc = backward(n - BLOCK, gs, acc, 0, True)

        gs, acc = lax.fori_loop(
            0,
            blocks - 2,
            lambda i, c: backward(pl.multiple_of((blocks - 2 - i) * BLOCK, BLOCK), *c, 0, False),
            (gs, acc),
        )
        send(grad_s, grad_hbm, BLOCK // SUB, (n - p.top) // SUB, g, 3 * g + 1)
        gs, acc = backward(0, gs, acc, H, False)
        for l in range(L):
            for k in range(K + 1):
                st_ref[p.acc + l * (K + 1) + k, lanes, :] = acc[l][k]
        for (kind, l, t), i in p.state.items():
            if kind == "a":
                st_ref[i, lanes, :] = a_s[l - 1][t, lanes, :]
            elif kind == "d":
                st_ref[i, lanes, :] = d_s[l][t, lanes, :]
            elif kind == "x":
                st_ref[i, lanes, :] = x_ref[tile(0, t)]
            elif kind == "ct":
                st_ref[i, lanes, :] = ct_ref[tile(0, t)]
            elif kind == "out":
                st_ref[i, lanes, :] = out_s[tile(0, t)]
            elif kind == "grad":
                st_ref[i, lanes, :] = grad_s[tile(0, t)]
    for copy in copies:
        copy.wait()


def border(p, keep_ref, st_ref, wb_ref, up_ref, edge_ref, ret_ref, sums_ref):
    L, R, H, K, M = p.layers, p.reach, p.halo, p.taps, p.late
    size = L * (K + 1) * SUB
    tiles = p.top // SUB
    keep = keep_ref[...]
    for g in range(p.groups):
        lanes = pl.ds(g * SUB, SUB)
        wb = [[wb_ref[l * (K + 1) + k, lanes, :] for k in range(K + 1)] for l in range(L)]
        wt = [w[:K][::-1] for w in wb]
        acc = [[st_ref[p.acc + l * (K + 1) + k, lanes, :] for k in range(K + 1)] for l in range(L)]
        state = lambda kind, l, t: st_ref[p.state[kind, l, t], lanes, :]

        def put(plane, t, value):
            where = (plane * tiles + t // SUB, pl.ds(g * SUB * SUB + t % SUB, SUB, stride=SUB), slice(None))
            edge_ref[where] = value

        act = [dict() for _ in range(L + 1)]
        kept = [dict() for _ in range(L + 1)]
        d = [dict() for _ in range(L)]
        for t in range(-M - H, H):
            act[0][t] = up_ref[up_ref.shape[0] + t, lanes, :] if t < 0 else state("x", 0, t)

        def past(l, t):
            rows = range(t - R, t + 1)
            if t < 0:
                return [act[l][s] for s in rows]
            return [kept[l][s] if s < 0 else act[l][s] for s in rows]

        for l in range(L):
            for t in range(-R, 0):
                kept[l][t] = act[l][t] * keep
            for t in range(-M - H + (l + 1) * R, (l + 1) * R):
                act[l + 1][t], d[l][t] = gate(conv(wb[l], past(l, t)))
            if l < L - 1:
                for t in range((l + 1) * R, H):
                    act[l + 1][t], d[l][t] = state("a", l + 1, t), state("d", l, t)
        for t in range(p.top):
            put(0, t, act[L][t] if t < H else state("out", 0, t))

        pre = [{t: state("g", l, t) for t in range(H, H + R)} for l in range(L)]
        for t in reversed(range(-M, H)):
            if t == -1:
                for l in range(L):
                    for s in range(R):
                        pre[l][s] = ret_ref[l * R + s, lanes, :]
            grad = up_ref[M + t, lanes, :] if t < 0 else state("ct", 0, t)
            for l in reversed(range(L)):
                pre[l][t] = grad * d[l][t]
                if 0 <= t < R:
                    ret_ref[l * R + t, lanes, :] = pre[l][t] * keep
                if t >= -(L - 1 - l) * R:
                    window = past(l, t)
                    for k in range(K):
                        acc[l][k] = acc[l][k] + pre[l][t] * window[k]
                    acc[l][K] = acc[l][K] + pre[l][t]
                if t >= 0 or l > 0:
                    grad = conv(wt[l], [pre[l][t + k] for k in range(K)])
            if t >= 0:
                put(1, t, grad)
        for t in range(H, p.top):
            put(1, t, state("grad", 0, t))

        for l in range(L):
            for k in range(K):
                sums_ref[pl.ds(g * size + l * SUB * K + k, SUB, stride=K), :] = 0.5 * acc[l][k]
            sums_ref[pl.ds(g * size + L * SUB * K + l * SUB, SUB), :] = 0.5 * acc[l][K]


def edges(p, out_in, grad_in, edge_ref, st_ref, wb_ref, ret_ref, out_ref, grad_ref, low_s, sem):
    tiles, L, R, K, n = p.top // SUB, p.layers, p.reach, p.taps, p.n
    copies = [
        pltpu.make_async_copy(edge_ref.at[pl.ds(0, tiles)], out_ref.at[pl.ds(0, tiles)], sem.at[0]),
        pltpu.make_async_copy(edge_ref.at[pl.ds(tiles, tiles)], grad_ref.at[pl.ds(0, tiles)], sem.at[1]),
        pltpu.make_async_copy(low_s, grad_ref.at[pl.ds(n // SUB - tiles, tiles)], sem.at[2]),
    ]
    copies[0].start()
    copies[1].start()
    for g in range(p.groups):
        lanes = pl.ds(g * SUB, SUB)
        state = lambda kind, l, t: st_ref[p.state[kind, l, t], lanes, :]
        grad = {}
        for l in reversed(range(L)):
            wt = [wb_ref[l * (K + 1) + k, lanes, :] for k in reversed(range(K))]
            low = n - (L - 1 - l) * R
            pre = {n + s: ret_ref[l * R + s, lanes, :] for s in range(R)}
            for t in range(low - R, n):
                pre[t] = grad[t] * state("d", l, t) if t >= low else state("g", l, t)
            grad = {t: conv(wt, [pre[t + k] for k in range(K)]) for t in range(low - R, n)}
        for i in range(p.top):
            t = n - p.top + i
            row = grad[t] if t in grad else state("grad", 0, t)
            low_s[i // SUB, pl.ds(g * SUB * SUB + i % SUB, SUB, stride=SUB), :] = row
    copies[2].start()
    for copy in copies:
        copy.wait()


def finish(p, mine_ref, theirs_ref, w_ref, b_ref):
    L, K = p.layers, p.taps
    size = L * (K + 1) * SUB
    for g in range(p.groups):
        for l in range(L):
            for rows, where in ((SUB * K, l * SUB * K), (SUB, L * SUB * K + l * SUB)):
                there = pl.ds(g * size + where, rows)
                total = mine_ref[there, :] + theirs_ref[there, :]
                if rows == SUB * K:
                    w_ref[pl.ds((l * p.cols + g * SUB) * K, rows), :] = total
                else:
                    for c in range(SUB):
                        at = (g * SUB + c) * LANES
                        b_ref[l : l + 1, at : at + LANES] = total[c : c + 1, :]


def shifted(array, axis, by):
    devices = lax.axis_size(axis)
    return lax.ppermute(array, axis, [(i, (i + by) % devices) for i in range(devices)])


def swapped(array, axis, bit):
    return lax.ppermute(array, axis, [(i, i ^ bit) for i in range(lax.axis_size(axis))])


def summed_but_one(array, axis):
    devices = lax.axis_size(axis)
    bits = [1 << i for i in range(devices.bit_length() - 1)]
    if len(bits) > 2:
        one, two = bits[:2]
        near = swapped(array, axis, one)
        far = swapped(array, axis, two)
        both = swapped(array, axis, one ^ two)
        array = (array + near) + (far + both)
        bits = bits[2:]
    for bit in bits[:-1]:
        array = array + swapped(array, axis, bit)
    return array, swapped(array, axis, bits[-1])


def tiled(a):
    n, width = a.shape
    return a.reshape(n // SUB, SUB, width // LANES, LANES).transpose(0, 2, 1, 3).reshape(n // SUB, -1, LANES)


def untiled(a, n, width):
    return a.reshape(n // SUB, width // LANES, SUB, LANES).transpose(0, 2, 1, 3).reshape(n, width)


def shards(inputs, conv_weight, conv_bias, cotangent):
    n, width = inputs.shape
    layers, taps = conv_weight.shape[:2]
    p = Plan(n, width, layers, taps)
    L, K, H, cols = layers, taps, p.halo, p.cols
    f32 = lambda *shape: jax.ShapeDtypeStruct(shape, jnp.float32)
    vmem, hbm = pl.BlockSpec(memory_space=pltpu.VMEM), pl.BlockSpec(memory_space=pltpu.HBM)

    shape = (n // SUB, cols * SUB, LANES)
    per_row = (n, cols, LANES)
    work = n * width
    cost = lambda flops: pl.CostEstimate(flops=flops * work, bytes_accessed=0, transcendentals=0)
    params = lambda mib: pltpu.CompilerParams(vmem_limit_bytes=mib << 20)
    x, ct = tiled(inputs), tiled(cotangent)
    weights = conv_weight.reshape(L, K, cols, LANES).transpose(0, 2, 1, 3).reshape(L * cols * K, LANES)

    M = p.late
    low, high = -(-M // SUB) * SUB, -(-(M + H) // SUB) * SUB
    spot = lax.broadcasted_iota(jnp.int32, (low + high, width), 0)
    rows = jnp.where(
        spot < low, jnp.pad(cotangent[n - low :], ((0, high), (0, 0))), inputs[n - low - high :]
    ).reshape(-1, cols, LANES)
    from_before = shifted(rows[low - M :], "seq", 1)

    out, grad, st, wb = pl.pallas_call(
        functools.partial(interior, p),
        out_shape=(f32(*shape), f32(*shape), f32(p.state_rows, cols, LANES), f32(L * (K + 1), cols, LANES)),
        in_specs=[vmem] * 4,
        out_specs=(hbm, hbm, vmem, vmem),
        scratch_shapes=[pltpu.VMEM(per_row, jnp.float32)] * (2 * L - 1)
        + [pltpu.VMEM(shape, jnp.float32)] * 2
        + [pltpu.SemaphoreType.DMA((3 * p.groups,))],
        compiler_params=params(24),
        cost_estimate=cost(90),
        name="interior",
    )(x, ct, weights, conv_bias.reshape(L, cols, LANES))

    keep = jnp.where(lax.axis_index("seq") == 0, 0.0, 1.0) * jnp.ones((SUB, LANES), jnp.float32)
    edge, ret, sums = pl.pallas_call(
        functools.partial(border, p),
        out_shape=(
            f32(2 * p.top // SUB, *shape[1:]),
            f32(H, cols, LANES),
            f32(L * (K + 1) * cols, LANES),
        ),
        in_specs=[vmem] * 4,
        out_specs=(vmem,) * 3,
        compiler_params=params(8),
        cost_estimate=cost(10),
        name="border",
    )(keep, st, wb, from_before)
    mine, theirs = summed_but_one(sums, "seq")
    returned = shifted(ret, "seq", -1)

    out, grad = pl.pallas_call(
        functools.partial(edges, p),
        out_shape=(f32(*shape), f32(*shape)),
        in_specs=[hbm, hbm] + [vmem] * 4,
        out_specs=(hbm, hbm),
        scratch_shapes=[
            pltpu.VMEM((p.top // SUB, *shape[1:]), jnp.float32),
            pltpu.SemaphoreType.DMA((3,)),
        ],
        input_output_aliases={0: 0, 1: 1},
        compiler_params=params(4),
        cost_estimate=cost(5),
        name="edges",
    )(out, grad, edge, st, wb, returned)

    w_sum, b_sum = pl.pallas_call(
        functools.partial(finish, p),
        out_shape=(f32(*weights.shape), f32(L, width)),
        in_specs=[vmem] * 2,
        out_specs=(vmem, vmem),
        compiler_params=params(4),
        cost_estimate=cost(5),
        name="finish",
    )(mine, theirs)
    return (
        untiled(out, n, width),
        untiled(grad, n, width),
        w_sum.reshape(L, cols, K, LANES).transpose(0, 2, 1, 3).reshape(L, K, width),
        b_sum,
    )


def solution(mesh):
    in_specs = (P("seq", "chan"), P(None, None, "chan"), P(None, "chan"), P("seq", "chan"))
    out_specs = (P("seq", "chan"), P("seq", "chan"), P(None, None, "chan"), P(None, "chan"))
    return jax.shard_map(shards, mesh=mesh, in_specs=in_specs, out_specs=out_specs, check_vma=False)
```

profile of v0, /device:TPU:0, one launch (start us, length us, event | category | flops | bytes accessed | tf_op | source)
XLA Modules:
  0.0 30.0 jit_solution(2442666671181365790)
XLA Ops:
  0.6 0.1 slice.16
  0.7 0.0 slice-start.1
  0.7 0.0 slice-start
  0.7 0.0 copy-start
  0.7 0.8 %slice-done.1 = f32[8,2048]{1,0:T(8,128)S(1)} async-done(((f32[128,2048]{1,0:T(8,128)}), f32[8,2048]{1,0:T(8,128)S(1)}, s32[]{:S(2)}) %slice-start.1) | async-done | bytes 65560 | tf_op jit(solution)/shard_map/slice | solution.py:342
  1.6 0.1 slice-done
  1.7 0.1 slice_select_fusion
  1.8 0.0 copy-start.3
  1.8 0.0 copy-start.2
  1.9 3.0 %collective-permute-start = (f32[22,16,128]{2,1,0:T(8,128)S(1)}, f32[22,16,128]{2,1,0:T(8,128)S(1)}, u32[]{:S(2)}, u32[]{:S(2)}) collective-permute-start(f32[22,16,128]{2,1,0:T(8,128)S(1)} %slice.18), channel_id=1, source_target_pairs={{0,4},{4,8},{8,12},{12,16},{16,20},{20,24},{24,28},{28,0},{1,5},{5... | collective-permute-start | bytes 540680 | tf_op jit(solution)/shard_map/ppermute | solution.py:291
  4.9 0.0 copy-done.3
  4.9 0.0 copy-done
  4.9 0.0 copy-done.2
  4.9 0.0 copy-start.1
  4.9 1.2 %copy-done.1 = f32[128,2048]{1,0:T(8,128)S(1)} copy-done((f32[128,2048]{1,0:T(8,128)S(1)}, f32[128,2048]{1,0:T(8,128)}, u32[]{:S(2)}) %copy-start.1) | copy-done | bytes 1048600
  6.2 4.5 %interior.1 = (f32[16,128,128]{2,1,0:T(8,128)}, f32[16,128,128]{2,1,0:T(8,128)}, f32[99,16,128]{2,1,0:T(8,128)S(1)}, f32[15,16,128]{2,1,0:T(8,128)S(1)}) custom-call(f32[16,128,128]{2,1,0:T(8,128)S(1)} %bitcast.37, f32[16,128,128]{2,1,0:T(8,128)S(1)} %bitcast.38, f32[192,128]{1,0:T(8,128)S(1)} %bitcast.40, f32[3,16,128]{2,1,0:T(8,128)S(1)} %bitcast.39), custom_call_target="tpu_custom_call" | custom-call | flops 23592960 | tf_op jit(solution)/shard_map/interior/pallas_call | solution.py:346
  10.7 1.8 %collective-permute-done.up_ref = f32[22,16,128]{2,1,0:T(8,128)S(1)} collective-permute-done((f32[22,16,128]{2,1,0:T(8,128)S(1)}, f32[22,16,128]{2,1,0:T(8,128)S(1)}, u32[]{:S(2)}, u32[]{:S(2)}) %collective-permute-start) | collective-permute-done | bytes 180256 | tf_op jit(solution)/shard_map/ppermute | solution.py:291
  12.5 0.4 %border.1 = (f32[4,128,128]{2,1,0:T(8,128)S(1)}, f32[9,16,128]{2,1,0:T(8,128)S(1)}, f32[240,128]{1,0:T(8,128)S(1)}) custom-call(f32[8,128]{1,0:T(8,128)S(1)} %mul.3.keep_ref, f32[99,16,128]{2,1,0:T(8,128)S(1)} %get-tuple-element.17.st_ref, f32[15,16,128]{2,1,0:T(8,128)S(1)} %get-tuple-element.18.wb_ref, f32[22,16,128]{2,1,0:T(8,128)S(1)} %collective-permute-done.up_ref), custom_call_target="tpu_custom_call" | custom-call | flops 2621440 | tf_op jit(solution)/shard_map/border/pallas_call | solution.py:360
  12.9 0.8 %collective-permute-start.4 = (f32[240,128]{1,0:T(8,128)S(1)}, f32[240,128]{1,0:T(8,128)S(1)}, u32[]{:S(2)}, u32[]{:S(2)}) collective-permute-start(f32[240,128]{1,0:T(8,128)S(1)} %get-tuple-element.23), channel_id=1, source_target_pairs={{0,12},{4,8},{8,4},{12,0},{16,28},{20,24},{24,20},{28,16},{1,13},{... | collective-permute-start | bytes 368648 | tf_op jit(solution)/shard_map/ppermute | solution.py:295
  13.7 0.4 %collective-permute-start.3 = (f32[240,128]{1,0:T(8,128)S(1)}, f32[240,128]{1,0:T(8,128)S(1)}, u32[]{:S(2)}, u32[]{:S(2)}) collective-permute-start(f32[240,128]{1,0:T(8,128)S(1)} %get-tuple-element.23), channel_id=1, source_target_pairs={{0,8},{4,12},{8,0},{12,4},{16,24},{20,28},{24,16},{28,20},{1,9},{5... | collective-permute-start | bytes 368648 | tf_op jit(solution)/shard_map/ppermute | solution.py:295
  14.1 2.3 %collective-permute-start.2 = (f32[240,128]{1,0:T(8,128)S(1)}, f32[240,128]{1,0:T(8,128)S(1)}, u32[]{:S(2)}, u32[]{:S(2)}) collective-permute-start(f32[240,128]{1,0:T(8,128)S(1)} %get-tuple-element.23), channel_id=1, source_target_pairs={{0,4},{4,0},{8,12},{12,8},{16,20},{20,16},{24,28},{28,24},{1,5},{5... | collective-permute-start | bytes 368648 | tf_op jit(solution)/shard_map/ppermute | solution.py:295
  16.4 3.2 %collective-permute-done.4 = f32[240,128]{1,0:T(8,128)S(1)} collective-permute-done((f32[240,128]{1,0:T(8,128)S(1)}, f32[240,128]{1,0:T(8,128)S(1)}, u32[]{:S(2)}, u32[]{:S(2)}) %collective-permute-start.4) | collective-permute-done | bytes 122912 | tf_op jit(solution)/shard_map/ppermute | solution.py:295
  19.6 0.0 collective-permute-done.3
  19.6 1.3 %collective-permute-done.2 = f32[240,128]{1,0:T(8,128)S(1)} collective-permute-done((f32[240,128]{1,0:T(8,128)S(1)}, f32[240,128]{1,0:T(8,128)S(1)}, u32[]{:S(2)}, u32[]{:S(2)}) %collective-permute-start.2) | collective-permute-done | bytes 122912 | tf_op jit(solution)/shard_map/ppermute | solution.py:295
  21.0 1.3 %collective-permute-start.5 = (f32[240,128]{1,0:T(8,128)S(1)}, f32[240,128]{1,0:T(8,128)S(1)}, u32[]{:S(2)}, u32[]{:S(2)}) collective-permute-start(f32[240,128]{1,0:T(8,128)S(1)} %add_add_fusion.mine_ref), channel_id=1, source_target_pairs={{0,16},{4,20},{8,24},{12,28},{16,0},{20,4},{24,8},{28,12},{1,17},{... | collective-permute-start | bytes 368648 | tf_op jit(solution)/shard_map/ppermute | solution.py:295
  22.3 2.2 %collective-permute-start.1 = (f32[9,16,128]{2,1,0:T(8,128)S(1)}, f32[9,16,128]{2,1,0:T(8,128)S(1)}, u32[]{:S(2)}, u32[]{:S(2)}) collective-permute-start(f32[9,16,128]{2,1,0:T(8,128)S(1)} %get-tuple-element.20), channel_id=1, source_target_pairs={{0,28},{4,0},{8,4},{12,8},{16,12},{20,16},{24,20},{28,24},{1,29},{... | collective-permute-start | bytes 221192 | tf_op jit(solution)/shard_map/ppermute | solution.py:291
  24.5 2.2 %collective-permute-done.1.ret_ref = f32[9,16,128]{2,1,0:T(8,128)S(1)} collective-permute-done((f32[9,16,128]{2,1,0:T(8,128)S(1)}, f32[9,16,128]{2,1,0:T(8,128)S(1)}, u32[]{:S(2)}, u32[]{:S(2)}) %collective-permute-start.1) | collective-permute-done | bytes 73760 | tf_op jit(solution)/shard_map/ppermute | solution.py:291
  26.7 0.8 %edges.1 = (f32[16,128,128]{2,1,0:T(8,128)}, f32[16,128,128]{2,1,0:T(8,128)}) custom-call(f32[16,128,128]{2,1,0:T(8,128)} %get-tuple-element.15.out_in, f32[16,128,128]{2,1,0:T(8,128)} %get-tuple-element.16.grad_in, f32[4,128,128]{2,1,0:T(8,128)S(1)} %get-tuple-element.19.edge_ref, ...), custom_call_target="tpu_custom_call", output_to_operand_aliasing={{0}: (0, {}), {1}: (1, {})} | custom-call | flops 1310720 | tf_op jit(solution)/shard_map/edges/pallas_call | solution.py:376
  27.4 1.9 %collective-permute-done.5.theirs_ref = f32[240,128]{1,0:T(8,128)S(1)} collective-permute-done((f32[240,128]{1,0:T(8,128)S(1)}, f32[240,128]{1,0:T(8,128)S(1)}, u32[]{:S(2)}, u32[]{:S(2)}) %collective-permute-start.5) | collective-permute-done | bytes 122912 | tf_op jit(solution)/shard_map/ppermute | solution.py:295
  29.3 0.7 %finish.1 = (f32[192,128]{1,0:T(8,128)}, f32[3,2048]{1,0:T(4,128)}) custom-call(f32[240,128]{1,0:T(8,128)S(1)} %add_add_fusion.mine_ref, f32[240,128]{1,0:T(8,128)S(1)} %collective-permute-done.5.theirs_ref), custom_call_target="tpu_custom_call" | custom-call | flops 1310720 | tf_op jit(solution)/shard_map/finish/pallas_call | solution.py:391
  (6 shorter events, 0.1 us)
Async XLA Ops:
  0.7 0.8 %slice-start.1 = ((f32[128,2048]{1,0:T(8,128)}), f32[8,2048]{1,0:T(8,128)S(1)}, s32[]{:S(2)}) async-start(f32[128,2048]{1,0:T(8,128)} %param.7), calls=%async_computation.1 | async-start | bytes 131072 | tf_op jit(solution)/shard_map/slice | solution.py:342
  0.7 1.0 %slice-start = ((f32[128,2048]{1,0:T(8,128)}), f32[24,2048]{1,0:T(8,128)S(1)}, s32[]{:S(2)}) async-start(f32[128,2048]{1,0:T(8,128)} %param.4), calls=%async_computation | async-start | bytes 393216 | tf_op jit(solution)/shard_map/slice | solution.py:342
  0.7 4.2 %copy-start = (f32[128,2048]{1,0:T(8,128)S(1)}, f32[128,2048]{1,0:T(8,128)}, u32[]{:S(2)}) copy-start(f32[128,2048]{1,0:T(8,128)} %param.4) | copy-start | bytes 3145732
  1.8 3.1 %copy-start.3 = (f32[3,2048]{1,0:T(4,128)S(1)}, f32[3,2048]{1,0:T(4,128)}, u32[]{:S(2)}) copy-start(f32[3,2048]{1,0:T(4,128)} %param.6) | copy-start | bytes 73732
  1.8 3.1 %copy-start.2 = (f32[3,4,2048]{2,1,0:T(4,128)S(1)}, f32[3,4,2048]{2,1,0:T(4,128)}, u32[]{:S(2)}) copy-start(f32[3,4,2048]{2,1,0:T(4,128)} %param.5) | copy-start | bytes 294916
  1.9 10.6 %collective-permute-start = (f32[22,16,128]{2,1,0:T(8,128)S(1)}, f32[22,16,128]{2,1,0:T(8,128)S(1)}, u32[]{:S(2)}, u32[]{:S(2)}) collective-permute-start(f32[22,16,128]{2,1,0:T(8,128)S(1)} %slice.18), channel_id=1, source_target_pairs={{0,4},{4,8},{8,12},{12,16},{16,20},{20,24},{24,28},{28,0},{1,5},{5... | collective-permute-start | bytes 540680 | tf_op jit(solution)/shard_map/ppermute | solution.py:291
  4.9 1.2 %copy-start.1 = (f32[128,2048]{1,0:T(8,128)S(1)}, f32[128,2048]{1,0:T(8,128)}, u32[]{:S(2)}) copy-start(f32[128,2048]{1,0:T(8,128)} %param.7) | copy-start | bytes 3145732
  12.9 6.8 %collective-permute-start.4 = (f32[240,128]{1,0:T(8,128)S(1)}, f32[240,128]{1,0:T(8,128)S(1)}, u32[]{:S(2)}, u32[]{:S(2)}) collective-permute-start(f32[240,128]{1,0:T(8,128)S(1)} %get-tuple-element.23), channel_id=1, source_target_pairs={{0,12},{4,8},{8,4},{12,0},{16,28},{20,24},{24,20},{28,16},{1,13},{... | collective-permute-start | bytes 368648 | tf_op jit(solution)/shard_map/ppermute | solution.py:295
  13.7 5.9 %collective-permute-start.3 = (f32[240,128]{1,0:T(8,128)S(1)}, f32[240,128]{1,0:T(8,128)S(1)}, u32[]{:S(2)}, u32[]{:S(2)}) collective-permute-start(f32[240,128]{1,0:T(8,128)S(1)} %get-tuple-element.23), channel_id=1, source_target_pairs={{0,8},{4,12},{8,0},{12,4},{16,24},{20,28},{24,16},{28,20},{1,9},{5... | collective-permute-start | bytes 368648 | tf_op jit(solution)/shard_map/ppermute | solution.py:295
  14.1 6.8 %collective-permute-start.2 = (f32[240,128]{1,0:T(8,128)S(1)}, f32[240,128]{1,0:T(8,128)S(1)}, u32[]{:S(2)}, u32[]{:S(2)}) collective-permute-start(f32[240,128]{1,0:T(8,128)S(1)} %get-tuple-element.23), channel_id=1, source_target_pairs={{0,4},{4,0},{8,12},{12,8},{16,20},{20,16},{24,28},{28,24},{1,5},{5... | collective-permute-start | bytes 368648 | tf_op jit(solution)/shard_map/ppermute | solution.py:295
  21.0 8.3 %collective-permute-start.5 = (f32[240,128]{1,0:T(8,128)S(1)}, f32[240,128]{1,0:T(8,128)S(1)}, u32[]{:S(2)}, u32[]{:S(2)}) collective-permute-start(f32[240,128]{1,0:T(8,128)S(1)} %add_add_fusion.mine_ref), channel_id=1, source_target_pairs={{0,16},{4,20},{8,24},{12,28},{16,0},{20,4},{24,8},{28,12},{1,17},{... | collective-permute-start | bytes 368648 | tf_op jit(solution)/shard_map/ppermute | solution.py:295
  22.3 4.4 %collective-permute-start.1 = (f32[9,16,128]{2,1,0:T(8,128)S(1)}, f32[9,16,128]{2,1,0:T(8,128)S(1)}, u32[]{:S(2)}, u32[]{:S(2)}) collective-permute-start(f32[9,16,128]{2,1,0:T(8,128)S(1)} %get-tuple-element.20), channel_id=1, source_target_pairs={{0,28},{4,0},{8,4},{12,8},{16,12},{20,16},{24,20},{28,24},{1,29},{... | collective-permute-start | bytes 221192 | tf_op jit(solution)/shard_map/ppermute | solution.py:291
where the time goes:
time: 30.2 us; the launch traced here: 30 us
  waiting for transfers between devices  10.4 us (34%)
  starting transfers between devices  10.1 us (33%)
  Pallas kernels  6.34 us (21%)
  local copies, waits for them, and re-layouts  2.33 us (8%)
  between operations  0.72 us (2%)
    ppermute x4, waiting for transfers between devices, swapped(): lax.ppermute(array, axis, [(i, i ^ bit) for i in range(lax.axis_size(axis...  6.41 us
    ppermute x2, starting transfers between devices, shifted(): lax.ppermute(array, axis, [(i, (i + by) % devices) for i in range(devices)])  5.2 us
    ppermute x4, starting transfers between devices, swapped(): lax.ppermute(array, axis, [(i, i ^ bit) for i in range(lax.axis_size(axis...  4.88 us
    pallas_call x1, Pallas kernels, shards(): pl.pallas_call(functools.partial(interior, p), out_shape=(f32(*shape), f3...  4.53 us
    ppermute x2, waiting for transfers between devices, shifted(): lax.ppermute(array, axis, [(i, (i + by) % devices) for i in range(devices)])  4 us
    unnamed x10, local copies, waits for them, and re-layouts  1.28 us
    slice x2, local copies, waits for them, and re-layouts, shards(): cotangent[n - low:]  0.84 us
    pallas_call x1, Pallas kernels, shards(): pl.pallas_call(functools.partial(edges, p), out_shape=(f32(*shape), f32(*...  0.77 us
  transfers between devices with their start and end apart: 6, of which 5 were waited for; matrix products, arithmetic and copies ran while one was open for 0% of the time, Pallas kernels for 18%

commit v1 on v0

--- a/solution.py
+++ b/solution.py
@@ -337,11 +337,12 @@
 
     M = p.late
     low, high = -(-M // SUB) * SUB, -(-(M + H) // SUB) * SUB
+    skip = high - M - H
     spot = lax.broadcasted_iota(jnp.int32, (low + high, width), 0)
     rows = jnp.where(
-        spot < low, jnp.pad(cotangent[n - low :], ((0, high), (0, 0))), inputs[n - low - high :]
+        spot < low + skip, jnp.pad(cotangent[n - low :], ((skip, high - skip), (0, 0))), inputs[n - low - high :]
     ).reshape(-1, cols, LANES)
-    from_before = shifted(rows[low - M :], "seq", 1)
+    from_before = shifted(rows[low + skip - M :], "seq", 1)
 
     out, grad, st, wb = pl.pallas_call(
         functools.partial(interior, p),
@@ -371,7 +372,9 @@
         name="border",
     )(keep, st, wb, from_before)
     mine, theirs = summed_but_one(sums, "seq")
-    returned = shifted(ret, "seq", -1)
+    size, wide = lax.axis_size("seq"), lax.axis_size("chan")
+    hops = [(i * wide + c, (i - 1) % size * wide + (c ^ 1 if i == 0 and wide % 2 == 0 else c)) for i in range(size) for c in range(wide)]
+    returned = lax.ppermute(ret, ("seq", "chan"), hops)
 
     out, grad = pl.pallas_call(
         functools.partial(edges, p),

time: 30.2 us -> 30.1 us (level)
  starting transfers between devices: 10.1 us -> 9.05 us
  waiting for transfers between devices: 10.4 us -> 11.4 us
    ppermute x0 -> x1, waiting for transfers between devices: none -> 3.41 us  [shards(): returned = lax.ppermute(ret, ('seq', 'chan'), hops)]
    ppermute x2 -> x1, waiting for transfers between devices: 4 us -> 1.62 us  [shifted(): lax.ppermute(array, axis, [(i, (i + by) % devices) for i in range(devices)])]
    ppermute x2 -> x1, starting transfers between devices: 5.2 us -> 3.05 us  [shifted(): lax.ppermute(array, axis, [(i, (i + by) % devices) for i in range(devices)])]
    ppermute x0 -> x1, starting transfers between devices: none -> 0.94 us  [shards(): returned = lax.ppermute(ret, ('seq', 'chan'), hops)]
  transfers between devices with their start and end apart: 6 -> 6, of which waited for: 5 -> 6; matrix products, arithmetic and copies ran while one was open for 0% -> 0% of each run, Pallas kernels for 18% -> 18%
where the time goes in v1:
time: 30.1 us; the launch traced here: 29.9 us
  waiting for transfers between devices  11.4 us (38%)
  starting transfers between devices  9.05 us (30%)
  Pallas kernels  6.34 us (21%)
  local copies, waits for them, and re-layouts  2.33 us (8%)
  between operations  0.72 us (2%)
    ppermute x4, waiting for transfers between devices, swapped(): lax.ppermute(array, axis, [(i, i ^ bit) for i in range(lax.axis_size(axis...  6.34 us
    ppermute x4, starting transfers between devices, swapped(): lax.ppermute(array, axis, [(i, i ^ bit) for i in range(lax.axis_size(axis...  5.05 us
    pallas_call x1, Pallas kernels, shards(): pl.pallas_call(functools.partial(interior, p), out_shape=(f32(*shape), f3...  4.53 us
    ppermute x1, waiting for transfers between devices, shards(): returned = lax.ppermute(ret, ('seq', 'chan'), hops)  3.41 us
    ppermute x1, starting transfers between devices, shifted(): lax.ppermute(array, axis, [(i, (i + by) % devices) for i in range(devices)])  3.05 us
    ppermute x1, waiting for transfers between devices, shifted(): lax.ppermute(array, axis, [(i, (i + by) % devices) for i in range(devices)])  1.62 us
    unnamed x10, local copies, waits for them, and re-layouts  1.28 us
    ppermute x1, starting transfers between devices, shards(): returned = lax.ppermute(ret, ('seq', 'chan'), hops)  0.94 us
  transfers between devices with their start and end apart: 6, of which 6 were waited for; matrix products, arithmetic and copies ran while one was open for 0% of the time, Pallas kernels for 18%

profile of v1, /device:TPU:0, one launch (start us, length us, event | category | flops | bytes accessed | tf_op | source)
XLA Modules:
  0.0 29.9 jit_solution(9212958624531772574)
XLA Ops:
  0.6 0.1 slice.16
  0.7 0.0 slice-start.1
  0.7 0.0 slice-start
  0.7 0.0 copy-start
  0.7 0.8 %slice-done.1 = f32[8,2048]{1,0:T(8,128)S(1)} async-done(((f32[128,2048]{1,0:T(8,128)}), f32[8,2048]{1,0:T(8,128)S(1)}, s32[]{:S(2)}) %slice-start.1) | async-done | bytes 65560 | tf_op jit(solution)/shard_map/slice | solution.py:343
  1.6 0.1 slice-done
  1.7 0.1 slice_select_fusion
  1.8 0.0 copy-start.3
  1.8 0.0 copy-start.2
  1.9 3.0 %collective-permute-start = (f32[21,16,128]{2,1,0:T(8,128)S(1)}, f32[21,16,128]{2,1,0:T(8,128)S(1)}, u32[]{:S(2)}, u32[]{:S(2)}) collective-permute-start(f32[21,16,128]{2,1,0:T(8,128)S(1)} %slice.18), channel_id=1, source_target_pairs={{0,4},{4,8},{8,12},{12,16},{16,20},{20,24},{24,28},{28,0},{1,5},{5... | collective-permute-start | bytes 516104 | tf_op jit(solution)/shard_map/ppermute | solution.py:291
  4.9 0.0 copy-done.3
  4.9 0.0 copy-done
  4.9 0.0 copy-done.2
  4.9 0.0 copy-start.1
  4.9 1.2 %copy-done.1 = f32[128,2048]{1,0:T(8,128)S(1)} copy-done((f32[128,2048]{1,0:T(8,128)S(1)}, f32[128,2048]{1,0:T(8,128)}, u32[]{:S(2)}) %copy-start.1) | copy-done | bytes 1048600
  6.2 4.5 %interior.1 = (f32[16,128,128]{2,1,0:T(8,128)}, f32[16,128,128]{2,1,0:T(8,128)}, f32[99,16,128]{2,1,0:T(8,128)S(1)}, f32[15,16,128]{2,1,0:T(8,128)S(1)}) custom-call(f32[16,128,128]{2,1,0:T(8,128)S(1)} %bitcast.37, f32[16,128,128]{2,1,0:T(8,128)S(1)} %bitcast.38, f32[192,128]{1,0:T(8,128)S(1)} %bitcast.40, f32[3,16,128]{2,1,0:T(8,128)S(1)} %bitcast.39), custom_call_target="tpu_custom_call" | custom-call | flops 23592960 | tf_op jit(solution)/shard_map/interior/pallas_call | solution.py:347
  10.7 1.6 %collective-permute-done.up_ref = f32[21,16,128]{2,1,0:T(8,128)S(1)} collective-permute-done((f32[21,16,128]{2,1,0:T(8,128)S(1)}, f32[21,16,128]{2,1,0:T(8,128)S(1)}, u32[]{:S(2)}, u32[]{:S(2)}) %collective-permute-start) | collective-permute-done | bytes 172064 | tf_op jit(solution)/shard_map/ppermute | solution.py:291
  12.3 0.4 %border.1 = (f32[4,128,128]{2,1,0:T(8,128)S(1)}, f32[9,16,128]{2,1,0:T(8,128)S(1)}, f32[240,128]{1,0:T(8,128)S(1)}) custom-call(f32[8,128]{1,0:T(8,128)S(1)} %mul.3.keep_ref, f32[99,16,128]{2,1,0:T(8,128)S(1)} %get-tuple-element.17.st_ref, f32[15,16,128]{2,1,0:T(8,128)S(1)} %get-tuple-element.18.wb_ref, f32[21,16,128]{2,1,0:T(8,128)S(1)} %collective-permute-done.up_ref), custom_call_target="tpu_custom_call" | custom-call | flops 2621440 | tf_op jit(solution)/shard_map/border/pallas_call | solution.py:361
  12.7 1.0 %collective-permute-start.4 = (f32[240,128]{1,0:T(8,128)S(1)}, f32[240,128]{1,0:T(8,128)S(1)}, u32[]{:S(2)}, u32[]{:S(2)}) collective-permute-start(f32[240,128]{1,0:T(8,128)S(1)} %get-tuple-element.23), channel_id=1, source_target_pairs={{0,12},{4,8},{8,4},{12,0},{16,28},{20,24},{24,20},{28,16},{1,13},{... | collective-permute-start | bytes 368648 | tf_op jit(solution)/shard_map/ppermute | solution.py:295
  13.7 0.4 %collective-permute-start.3 = (f32[240,128]{1,0:T(8,128)S(1)}, f32[240,128]{1,0:T(8,128)S(1)}, u32[]{:S(2)}, u32[]{:S(2)}) collective-permute-start(f32[240,128]{1,0:T(8,128)S(1)} %get-tuple-element.23), channel_id=1, source_target_pairs={{0,8},{4,12},{8,0},{12,4},{16,24},{20,28},{24,16},{28,20},{1,9},{5... | collective-permute-start | bytes 368648 | tf_op jit(solution)/shard_map/ppermute | solution.py:295
  14.1 2.1 %collective-permute-start.2 = (f32[240,128]{1,0:T(8,128)S(1)}, f32[240,128]{1,0:T(8,128)S(1)}, u32[]{:S(2)}, u32[]{:S(2)}) collective-permute-start(f32[240,128]{1,0:T(8,128)S(1)} %get-tuple-element.23), channel_id=1, source_target_pairs={{0,4},{4,0},{8,12},{12,8},{16,20},{20,16},{24,28},{28,24},{1,5},{5... | collective-permute-start | bytes 368648 | tf_op jit(solution)/shard_map/ppermute | solution.py:295
  16.2 3.2 %collective-permute-done.4 = f32[240,128]{1,0:T(8,128)S(1)} collective-permute-done((f32[240,128]{1,0:T(8,128)S(1)}, f32[240,128]{1,0:T(8,128)S(1)}, u32[]{:S(2)}, u32[]{:S(2)}) %collective-permute-start.4) | collective-permute-done | bytes 122912 | tf_op jit(solution)/shard_map/ppermute | solution.py:295
  19.5 0.1 collective-permute-done.3
  19.5 1.2 %collective-permute-done.2 = f32[240,128]{1,0:T(8,128)S(1)} collective-permute-done((f32[240,128]{1,0:T(8,128)S(1)}, f32[240,128]{1,0:T(8,128)S(1)}, u32[]{:S(2)}, u32[]{:S(2)}) %collective-permute-start.2) | collective-permute-done | bytes 122912 | tf_op jit(solution)/shard_map/ppermute | solution.py:295
  20.8 1.5 %collective-permute-start.5 = (f32[240,128]{1,0:T(8,128)S(1)}, f32[240,128]{1,0:T(8,128)S(1)}, u32[]{:S(2)}, u32[]{:S(2)}) collective-permute-start(f32[240,128]{1,0:T(8,128)S(1)} %add_add_fusion.mine_ref), channel_id=1, source_target_pairs={{0,16},{4,20},{8,24},{12,28},{16,0},{20,4},{24,8},{28,12},{1,17},{... | collective-permute-start | bytes 368648 | tf_op jit(solution)/shard_map/ppermute | solution.py:295
  22.3 0.9 %collective-permute-start.1 = (f32[9,16,128]{2,1,0:T(8,128)S(1)}, f32[9,16,128]{2,1,0:T(8,128)S(1)}, u32[]{:S(2)}, u32[]{:S(2)}) collective-permute-start(f32[9,16,128]{2,1,0:T(8,128)S(1)} %get-tuple-element.20), channel_id=1, source_target_pairs={{0,29},{1,28},{2,31},{3,30},{4,0},{5,1},{6,2},{7,3},{8,4},{9,5},{1... | collective-permute-start | bytes 221192 | tf_op jit(solution)/shard_map/ppermute | solution.py:377
  23.3 3.4 %collective-permute-done.1.ret_ref = f32[9,16,128]{2,1,0:T(8,128)S(1)} collective-permute-done((f32[9,16,128]{2,1,0:T(8,128)S(1)}, f32[9,16,128]{2,1,0:T(8,128)S(1)}, u32[]{:S(2)}, u32[]{:S(2)}) %collective-permute-start.1) | collective-permute-done | bytes 73760 | tf_op jit(solution)/shard_map/ppermute | solution.py:377
  26.7 0.8 %edges.1 = (f32[16,128,128]{2,1,0:T(8,128)}, f32[16,128,128]{2,1,0:T(8,128)}) custom-call(f32[16,128,128]{2,1,0:T(8,128)} %get-tuple-element.15.out_in, f32[16,128,128]{2,1,0:T(8,128)} %get-tuple-element.16.grad_in, f32[4,128,128]{2,1,0:T(8,128)S(1)} %get-tuple-element.19.edge_ref, ...), custom_call_target="tpu_custom_call", output_to_operand_aliasing={{0}: (0, {}), {1}: (1, {})} | custom-call | flops 1310720 | tf_op jit(solution)/shard_map/edges/pallas_call | solution.py:379
  27.4 1.8 %collective-permute-done.5.theirs_ref = f32[240,128]{1,0:T(8,128)S(1)} collective-permute-done((f32[240,128]{1,0:T(8,128)S(1)}, f32[240,128]{1,0:T(8,128)S(1)}, u32[]{:S(2)}, u32[]{:S(2)}) %collective-permute-start.5) | collective-permute-done | bytes 122912 | tf_op jit(solution)/shard_map/ppermute | solution.py:295
  29.3 0.7 %finish.1 = (f32[192,128]{1,0:T(8,128)}, f32[3,2048]{1,0:T(4,128)}) custom-call(f32[240,128]{1,0:T(8,128)S(1)} %add_add_fusion.mine_ref, f32[240,128]{1,0:T(8,128)S(1)} %collective-permute-done.5.theirs_ref), custom_call_target="tpu_custom_call" | custom-call | flops 1310720 | tf_op jit(solution)/shard_map/finish/pallas_call | solution.py:394
  (6 shorter events, 0.1 us)
Async XLA Ops:
  0.7 0.8 %slice-start.1 = ((f32[128,2048]{1,0:T(8,128)}), f32[8,2048]{1,0:T(8,128)S(1)}, s32[]{:S(2)}) async-start(f32[128,2048]{1,0:T(8,128)} %param.7), calls=%async_computation.1 | async-start | bytes 131072 | tf_op jit(solution)/shard_map/slice | solution.py:343
  0.7 1.0 %slice-start = ((f32[128,2048]{1,0:T(8,128)}), f32[24,2048]{1,0:T(8,128)S(1)}, s32[]{:S(2)}) async-start(f32[128,2048]{1,0:T(8,128)} %param.4), calls=%async_computation | async-start | bytes 393216 | tf_op jit(solution)/shard_map/slice | solution.py:343
  0.7 4.2 %copy-start = (f32[128,2048]{1,0:T(8,128)S(1)}, f32[128,2048]{1,0:T(8,128)}, u32[]{:S(2)}) copy-start(f32[128,2048]{1,0:T(8,128)} %param.4) | copy-start | bytes 3145732
  1.8 3.1 %copy-start.3 = (f32[3,2048]{1,0:T(4,128)S(1)}, f32[3,2048]{1,0:T(4,128)}, u32[]{:S(2)}) copy-start(f32[3,2048]{1,0:T(4,128)} %param.6) | copy-start | bytes 73732
  1.8 3.1 %copy-start.2 = (f32[3,4,2048]{2,1,0:T(4,128)S(1)}, f32[3,4,2048]{2,1,0:T(4,128)}, u32[]{:S(2)}) copy-start(f32[3,4,2048]{2,1,0:T(4,128)} %param.5) | copy-start | bytes 294916
  1.9 10.5 %collective-permute-start = (f32[21,16,128]{2,1,0:T(8,128)S(1)}, f32[21,16,128]{2,1,0:T(8,128)S(1)}, u32[]{:S(2)}, u32[]{:S(2)}) collective-permute-start(f32[21,16,128]{2,1,0:T(8,128)S(1)} %slice.18), channel_id=1, source_target_pairs={{0,4},{4,8},{8,12},{12,16},{16,20},{20,24},{24,28},{28,0},{1,5},{5... | collective-permute-start | bytes 516104 | tf_op jit(solution)/shard_map/ppermute | solution.py:291
  4.9 1.2 %copy-start.1 = (f32[128,2048]{1,0:T(8,128)S(1)}, f32[128,2048]{1,0:T(8,128)}, u32[]{:S(2)}) copy-start(f32[128,2048]{1,0:T(8,128)} %param.7) | copy-start | bytes 3145732
  12.7 6.8 %collective-permute-start.4 = (f32[240,128]{1,0:T(8,128)S(1)}, f32[240,128]{1,0:T(8,128)S(1)}, u32[]{:S(2)}, u32[]{:S(2)}) collective-permute-start(f32[240,128]{1,0:T(8,128)S(1)} %get-tuple-element.23), channel_id=1, source_target_pairs={{0,12},{4,8},{8,4},{12,0},{16,28},{20,24},{24,20},{28,16},{1,13},{... | collective-permute-start | bytes 368648 | tf_op jit(solution)/shard_map/ppermute | solution.py:295
  13.7 5.8 %collective-permute-start.3 = (f32[240,128]{1,0:T(8,128)S(1)}, f32[240,128]{1,0:T(8,128)S(1)}, u32[]{:S(2)}, u32[]{:S(2)}) collective-permute-start(f32[240,128]{1,0:T(8,128)S(1)} %get-tuple-element.23), channel_id=1, source_target_pairs={{0,8},{4,12},{8,0},{12,4},{16,24},{20,28},{24,16},{28,20},{1,9},{5... | collective-permute-start | bytes 368648 | tf_op jit(solution)/shard_map/ppermute | solution.py:295
  14.1 6.6 %collective-permute-start.2 = (f32[240,128]{1,0:T(8,128)S(1)}, f32[240,128]{1,0:T(8,128)S(1)}, u32[]{:S(2)}, u32[]{:S(2)}) collective-permute-start(f32[240,128]{1,0:T(8,128)S(1)} %get-tuple-element.23), channel_id=1, source_target_pairs={{0,4},{4,0},{8,12},{12,8},{16,20},{20,16},{24,28},{28,24},{1,5},{5... | collective-permute-start | bytes 368648 | tf_op jit(solution)/shard_map/ppermute | solution.py:295
  20.8 8.4 %collective-permute-start.5 = (f32[240,128]{1,0:T(8,128)S(1)}, f32[240,128]{1,0:T(8,128)S(1)}, u32[]{:S(2)}, u32[]{:S(2)}) collective-permute-start(f32[240,128]{1,0:T(8,128)S(1)} %add_add_fusion.mine_ref), channel_id=1, source_target_pairs={{0,16},{4,20},{8,24},{12,28},{16,0},{20,4},{24,8},{28,12},{1,17},{... | collective-permute-start | bytes 368648 | tf_op jit(solution)/shard_map/ppermute | solution.py:295
  22.3 4.4 %collective-permute-start.1 = (f32[9,16,128]{2,1,0:T(8,128)S(1)}, f32[9,16,128]{2,1,0:T(8,128)S(1)}, u32[]{:S(2)}, u32[]{:S(2)}) collective-permute-start(f32[9,16,128]{2,1,0:T(8,128)S(1)} %get-tuple-element.20), channel_id=1, source_target_pairs={{0,29},{1,28},{2,31},{3,30},{4,0},{5,1},{6,2},{7,3},{8,4},{9,5},{1... | collective-permute-start | bytes 221192 | tf_op jit(solution)/shard_map/ppermute | solution.py:377
